TPU v7x, 512 devices: a whole 4x4x16 slice. The times are simulated.
512 devices in a mesh: dom: 512 (over z, y, x, core).
Axes of the slice: x: 4, y: 4, z: 16, core: 2. Of those that a mesh axis runs over, the one named last changes fastest.
Arguments:
- particles: float32 [512, 2, 256, 128], P('dom'), may hold values from -60 to 60
- offspring: int32 [512], P('dom'), may hold values from 0 to 7, as said below
- noise: float32 [2, 512, 2, 256, 128], P(None, 'dom'), may hold values from -6 to 6
- accept: int32 [2, 512], P(None, 'dom'), may hold values 0 or 1
- observed: float32 [256, 256], replicated, may hold values from -6 to 6
Outputs:
- moved: float32 [512, 2, 256, 128], P('dom')
- misfit: float32 [2, 512], P(None, 'dom')
Inputs may be any that keep to these rules, and one draw needn't show every extreme that they name: `offspring`: the counts sum to 512. Slot s, numbered by the counts' running sum, is filled by a particle at most 3 places from s, and in every draw some slot is filled from exactly 3 places away.
All inputs are finite; a program needn't handle non-finite values. No bound on the sum of `accept` on one device may be relied on, other than what follows from the above.
Results may differ from a plain program's by a relative error of at most 0.0001.
Values sent between devices are 32-bit elements; how exact they have to be, the bound alone decides.
No kernel may reach another device: no remote copies, remote signals or barrier semaphores. Data moves between devices by JAX's collectives and lax.ppermute only.
A program may use at most 64 MiB of HBM per device.

v0:
```python
import math
import jax
import jax.numpy as jnp
from jax import lax
from jax.sharding import PartitionSpec as P

MOVES = 2
SPAN = 3
LOW = 16
time_step = 0.05
viscosity = 0.001
noise_level = 0.5
spectral_scale = 64.0
prior_amplitude = 1.5
step_size = 0.4
highest = lax.Precision.HIGHEST


def carried_in(part, axis, combine, identity):
    place = lax.axis_index(axis)
    gathered = lax.all_gather(part, axis)
    state = jnp.zeros_like(part) + jnp.asarray(identity, part.dtype)

    def one(lap, state):
        return combine(state, lax.dynamic_index_in_dim(gathered, lap, 0, False))

    return lax.fori_loop(0, place, one, state)


def from_behind(value, axis, steps):
    count = lax.axis_size(axis)
    leading, last = (max(0, -steps), min(count, count - steps))
    return lax.ppermute(value, axis, [(source, source + steps) for source in range(leading, last)])


def tables(grid):
    half = grid // 2
    index_a = jnp.arange(grid)
    phase_y = (index_a[:, None] * index_a[None, :] % grid).astype(jnp.float32) * (
        2.0 * math.pi / grid
    )
    cos_y = jnp.cos(phase_y)
    sin_y = jnp.sin(phase_y)
    index_q = jnp.arange(half)
    phase_x = (index_q[:, None] * index_a[None, :] % grid).astype(jnp.float32) * (
        2.0 * math.pi / grid
    )
    weight = jnp.where(index_q == 0, 1.0, 2.0).astype(jnp.float32)[:, None]
    backward_table = (
        jnp.concatenate([weight * jnp.cos(phase_x), -weight * jnp.sin(phase_x)], axis=0)
        / spectral_scale
    )
    fore_table = jnp.concatenate([jnp.cos(phase_x).T, -jnp.sin(phase_x).T], axis=1) * (
        spectral_scale / (grid * grid)
    )
    return (cos_y, sin_y, backward_table, fore_table)


def synthesize(real_part, imag_part, lookup_tables):
    cos_y, sin_y, backward_table, fore_table = lookup_tables
    half = real_part.shape[-1]
    stacked = jnp.concatenate([real_part, imag_part], axis=-1)
    with_cos = jnp.einsum("ap,bpq->baq", cos_y, stacked, precision=highest)
    with_sin = jnp.einsum("ap,bpq->baq", sin_y, stacked, precision=highest)
    rows_re = with_cos[..., :half] - with_sin[..., half:]
    rows_im = with_sin[..., :half] + with_cos[..., half:]
    joined = jnp.concatenate([rows_re, rows_im], axis=-1)
    return jnp.einsum("baq,qc->bac", joined, backward_table, precision=highest)


def analyse(field, lookup_tables):
    cos_y, sin_y, backward_table, fore_table = lookup_tables
    half = field.shape[-1] // 2
    rows = jnp.einsum("bac,cq->baq", field, fore_table, precision=highest)
    with_cos = jnp.einsum("ap,baq->bpq", cos_y, rows, precision=highest)
    with_sin = jnp.einsum("ap,baq->bpq", sin_y, rows, precision=highest)
    return (
        with_cos[..., :half] + with_sin[..., half:],
        with_cos[..., half:] - with_sin[..., :half],
    )


def wavenumbers(grid):
    index_y = jnp.arange(grid)
    wave_y = jnp.where(index_y < grid // 2, index_y, index_y - grid).astype(jnp.float32)[:, None]
    wave_x = jnp.arange(grid // 2).astype(jnp.float32)[None, :]
    return (wave_y, wave_x)


def predicted_state(present_state, observed, lookup_tables):
    grid = present_state.shape[2]
    count = present_state.shape[0]
    wave_y, wave_x = wavenumbers(grid)
    wave_sq = wave_y * wave_y + wave_x * wave_x
    inverse_sq = jnp.where(wave_sq > 0, 1.0 / jnp.maximum(wave_sq, 1.0), 0.0)
    keeper = ((jnp.abs(wave_y) <= grid // 3) & (wave_x <= grid // 3)).astype(jnp.float32)
    damping = 1.0 + time_step * viscosity * wave_sq
    real_part = present_state[:, 0]
    imag_part = present_state[:, 1]
    psi_re = real_part * inverse_sq
    psi_im = imag_part * inverse_sq
    fields = synthesize(
        jnp.concatenate([real_part, -wave_y * psi_im, wave_x * psi_im], axis=0),
        jnp.concatenate([imag_part, wave_y * psi_re, -wave_x * psi_re], axis=0),
        lookup_tables,
    )
    vort = fields[:count]
    products = jnp.concatenate(
        [fields[count : 2 * count] * vort, fields[2 * count :] * vort], axis=0
    )
    flux_re, flux_im = analyse(products, lookup_tables)
    nonlin_re = -(wave_x * flux_im[:count] + wave_y * flux_im[count:]) * keeper
    nonlin_im = (wave_x * flux_re[:count] + wave_y * flux_re[count:]) * keeper
    real_part = (real_part - time_step * nonlin_re) / damping
    imag_part = (imag_part - time_step * nonlin_im) / damping
    final = synthesize(real_part, imag_part, lookup_tables)
    return jnp.sum((final - observed[None]) ** 2, axis=(1, 2)) / (
        2.0 * noise_level * noise_level * grid * grid
    )


def low_modes(block):
    grid = block.shape[-2]
    return jnp.concatenate(
        [block[..., : LOW // 2, :LOW], block[..., grid - LOW // 2 :, :LOW]], axis=-2
    )


def add_counts(earlier, later):
    return earlier + later


def body(particles, offspring, noise, accept, observed):
    per_device = particles.shape[0]
    grid = particles.shape[2]
    devices = lax.axis_size("dom")
    position = lax.axis_index("dom")
    before = carried_in(jnp.sum(offspring), "dom", add_counts, jnp.int32(0))
    finish = before + jnp.cumsum(offspring)
    starts = finish - offspring
    package = (particles, starts.astype(jnp.float32), finish.astype(jnp.float32))
    gathered_values = [package]
    for distance in range(1, SPAN + 1):
        for direction in (1, -1):
            gathered_values.append(
                from_behind((package[0], package[1], package[2]), "dom", direction * distance)
            )
    candidates = jnp.concatenate([item[0] for item in gathered_values], axis=0)
    cand_start = jnp.concatenate([item[1] for item in gathered_values], axis=0)
    cand_end = jnp.concatenate([item[2] for item in gathered_values], axis=0)
    slot_ids = (position * per_device + jnp.arange(per_device, dtype=jnp.int32)).astype(jnp.float32)
    chosen = (
        (cand_start[None, :] <= slot_ids[:, None]) & (slot_ids[:, None] < cand_end[None, :])
    ).astype(jnp.float32)
    present_state = jnp.einsum("sc,cxyz->sxyz", chosen, candidates, precision=highest)
    totals = lax.psum(jnp.sum(low_modes(present_state) ** 2, axis=0), "dom")
    adapted = jnp.sqrt(totals / (per_device * devices) + 1e-06)
    wave_y, wave_x = wavenumbers(grid)
    prior = prior_amplitude / (1.0 + jnp.sqrt(wave_y * wave_y + wave_x * wave_x) / 8.0)
    spread = jnp.stack([prior, prior])
    spread = spread.at[:, : LOW // 2, :LOW].set(adapted[:, : LOW // 2])
    spread = spread.at[:, grid - LOW // 2 :, :LOW].set(adapted[:, LOW // 2 :])
    lookup_tables = tables(grid)
    keep = math.sqrt(1.0 - step_size * step_size)
    score_values = []
    for move in range(MOVES):
        candidate_state = keep * present_state + step_size * spread[None] * noise[move]
        score_values.append(predicted_state(candidate_state, observed, lookup_tables))
        present_state = jnp.where(
            accept[move][:, None, None, None] == 1, candidate_state, present_state
        )
    return (present_state, jnp.stack(score_values))


def solution(mesh):
    return jax.shard_map(
        body,
        mesh=mesh,
        in_specs=(
            P("dom", None, None, None),
            P("dom"),
            P(None, "dom", None, None, None),
            P(None, "dom"),
            P(),
        ),
        out_specs=(P("dom", None, None, None), P(None, "dom")),
        check_vma=False,
    )
```

profile of v0, /device:TPU:1, one launch (start us, length us, event | category | flops | bytes accessed | tf_op | source)
XLA Modules:
  0.0 980.4 jit_solution(8580837013161240498)
XLA Ops:
  1.4 111.0 %all-reduce = s32[512]{0:T(512)S(1)} all-reduce(s32[512]{0:T(512)S(1)} %dynamic-update-slice.8), channel_id=1, replica_groups=mesh['dom'=512] {'dom'}, use_global_device_ids=true, to_apply=%add | all-reduce | flops 512 | bytes 4096
  113.7 8.1 collective-permute-start.10
  123.1 3.1 collective-permute-start.12
  126.2 1.9 collective-permute-start.13
  128.2 7.6 collective-permute-start.14
  141.4 3.9 collective-permute-start.6
  145.3 2.7 collective-permute-start.7
  148.1 6.3 collective-permute-start.8
  155.6 7.6 collective-permute-start
  163.2 2.8 collective-permute-start.1
  166.0 3.8 concatenate.77
  169.9 7.6 collective-permute-start.2
  178.7 11.9 %collective-permute-start.4 = (f32[1]{0:T(128)}, f32[1]{0:T(128)}, u32[]{:S(2)}, u32[]{:S(2)}) collective-permute-start(f32[1]{0:T(128)} %convert_element_type.174), channel_id=1, source_target_pairs={{0,3},{1,4},{2,5},{3,6},{4,7},{5,8},{6,9},{7,10},{8,11},{9,12},{10... | collective-permute-start | bytes 20 | tf_op jit(solution)/shard_map/ppermute | solution.py:33
  193.2 4.5 collective-permute-done.5
  197.7 9.1 collective-permute-start.16
  206.8 3.7 concatenate.76
  215.7 5.3 collective-permute-done.17
  221.0 2.1 fusion
  223.4 725.5 %psum.7 = f32[2,16,16]{1,2,0:T(8,128)S(1)} all-reduce(f32[2,16,16]{1,2,0:T(8,128)S(1)} %maximum_multiply_fusion.6), channel_id=1, replica_groups=mesh['dom'=512] {'dom'}, use_global_device_ids=true, to_apply=%region_2.3 | all-reduce | flops 512 | bytes 4096 | tf_op jit(solution)/shard_map/psum | solution.py:156
  951.2 1.8 convolution_bitcast_fusion.1
  953.0 1.8 convolution_bitcast_fusion
  957.1 1.6 convolution_bitcast_fusion.4
  960.2 1.8 convolution_bitcast_fusion.3
  962.0 2.0 convolution_bitcast_fusion.2
  (89 shorter events, 39.2 us)
Async XLA Ops:
  0.6 138.0 %copy-start.1 = (s32[2,1]{0,1:T(1,128)S(1)}, s32[2,1]{0,1:T(1,128)}, u32[]{:S(2)}) copy-start(s32[2,1]{0,1:T(1,128)} %param.14) | copy-start | bytes 28
  113.7 27.7 %collective-permute-start.10 = (f32[1]{0:T(128)}, f32[1]{0:T(128)}, u32[]{:S(2)}, u32[]{:S(2)}) collective-permute-start(f32[1]{0:T(128)} %convert_element_type.176), channel_id=1, source_target_pairs={{0,3},{1,4},{2,5},{3,6},{4,7},{5,8},{6,9},{7,10},{8,11},{9,12},{10... | collective-permute-start | bytes 20 | tf_op jit(solution)/shard_map/ppermute | solution.py:33
  121.8 23.5 %collective-permute-start.11 = (f32[1]{0:T(128)}, f32[1]{0:T(128)}, u32[]{:S(2)}, u32[]{:S(2)}) collective-permute-start(f32[1]{0:T(128)} %convert_element_type.176), channel_id=1, source_target_pairs={{3,0},{4,1},{5,2},{6,3},{7,4},{8,5},{9,6},{10,7},{11,8},{12,9},{13... | collective-permute-start | bytes 20 | tf_op jit(solution)/shard_map/ppermute | solution.py:33
  123.1 87.4 %collective-permute-start.12 = (f32[1,2,256,128]{3,2,1,0:T(8,128)}, f32[1,2,256,128]{3,2,1,0:T(8,128)}, u32[]{:S(2)}, u32[]{:S(2)}) collective-permute-start(f32[1,2,256,128]{3,2,1,0:T(8,128)} %param.11), channel_id=1, source_target_pairs={{0,1},{1,2},{2,3},{3,4},{4,5},{5,6},{6,7},{7,8},{8,9},{9,10},{10,1... | collective-permute-start | bytes 786440 | tf_op jit(solution)/shard_map/ppermute | solution.py:33
  126.2 86.5 %collective-permute-start.13 = (f32[1,2,256,128]{3,2,1,0:T(8,128)}, f32[1,2,256,128]{3,2,1,0:T(8,128)}, u32[]{:S(2)}, u32[]{:S(2)}) collective-permute-start(f32[1,2,256,128]{3,2,1,0:T(8,128)} %param.11), channel_id=1, source_target_pairs={{1,0},{2,1},{3,2},{4,3},{5,4},{6,5},{7,6},{8,7},{9,8},{10,9},{11,1... | collective-permute-start | bytes 786440 | tf_op jit(solution)/shard_map/ppermute | solution.py:33
  128.2 85.5 %collective-permute-start.14 = (f32[1,2,256,128]{3,2,1,0:T(8,128)}, f32[1,2,256,128]{3,2,1,0:T(8,128)}, u32[]{:S(2)}, u32[]{:S(2)}) collective-permute-start(f32[1,2,256,128]{3,2,1,0:T(8,128)} %param.11), channel_id=1, source_target_pairs={{0,2},{1,3},{2,4},{3,5},{4,6},{5,7},{6,8},{7,9},{8,10},{9,11},{10,... | collective-permute-start | bytes 786440 | tf_op jit(solution)/shard_map/ppermute | solution.py:33
  141.4 6.7 collective-permute-start.6
  145.3 9.0 collective-permute-start.7
  148.1 7.6 collective-permute-start.8
  154.3 8.9 collective-permute-start.9
  155.6 14.2 %collective-permute-start = (f32[1]{0:T(128)}, f32[1]{0:T(128)}, u32[]{:S(2)}, u32[]{:S(2)}) collective-permute-start(f32[1]{0:T(128)} %convert_element_type.174), channel_id=1, source_target_pairs={{0,1},{1,2},{2,3},{3,4},{4,5},{5,6},{6,7},{7,8},{8,9},{9,10},{10,1... | collective-permute-start | bytes 20 | tf_op jit(solution)/shard_map/ppermute | solution.py:33
  163.2 14.3 %collective-permute-start.1 = (f32[1]{0:T(128)}, f32[1]{0:T(128)}, u32[]{:S(2)}, u32[]{:S(2)}) collective-permute-start(f32[1]{0:T(128)} %convert_element_type.174), channel_id=1, source_target_pairs={{1,0},{2,1},{3,2},{4,3},{5,4},{6,5},{7,6},{8,7},{9,8},{10,9},{11,1... | collective-permute-start | bytes 20 | tf_op jit(solution)/shard_map/ppermute | solution.py:33
  169.9 8.9 collective-permute-start.2
  177.4 13.2 %collective-permute-start.3 = (f32[1]{0:T(128)}, f32[1]{0:T(128)}, u32[]{:S(2)}, u32[]{:S(2)}) collective-permute-start(f32[1]{0:T(128)} %convert_element_type.174), channel_id=1, source_target_pairs={{2,0},{3,1},{4,2},{5,3},{6,4},{7,5},{8,6},{9,7},{10,8},{11,9},{12,... | collective-permute-start | bytes 20 | tf_op jit(solution)/shard_map/ppermute | solution.py:33
  178.7 13.2 %collective-permute-start.4 = (f32[1]{0:T(128)}, f32[1]{0:T(128)}, u32[]{:S(2)}, u32[]{:S(2)}) collective-permute-start(f32[1]{0:T(128)} %convert_element_type.174), channel_id=1, source_target_pairs={{0,3},{1,4},{2,5},{3,6},{4,7},{5,8},{6,9},{7,10},{8,11},{9,12},{10... | collective-permute-start | bytes 20 | tf_op jit(solution)/shard_map/ppermute | solution.py:33
  190.6 7.1 collective-permute-start.5
  191.9 22.8 %collective-permute-start.15 = (f32[1,2,256,128]{3,2,1,0:T(8,128)}, f32[1,2,256,128]{3,2,1,0:T(8,128)S(1)}, u32[]{:S(2)}, u32[]{:S(2)}) collective-permute-start(f32[1,2,256,128]{3,2,1,0:T(8,128)} %param.11), channel_id=1, source_target_pairs={{2,0},{3,1},{4,2},{5,3},{6,4},{7,5},{8,6},{9,7},{10,8},{11,9},{12,... | collective-permute-start | bytes 786440 | tf_op jit(solution)/shard_map/ppermute | solution.py:33
  197.7 17.0 %collective-permute-start.16 = (f32[1,2,256,128]{3,2,1,0:T(8,128)}, f32[1,2,256,128]{3,2,1,0:T(8,128)}, u32[]{:S(2)}, u32[]{:S(2)}) collective-permute-start(f32[1,2,256,128]{3,2,1,0:T(8,128)} %param.11), channel_id=1, source_target_pairs={{0,3},{1,4},{2,5},{3,6},{4,7},{5,8},{6,9},{7,10},{8,11},{9,12},{10... | collective-permute-start | bytes 786440 | tf_op jit(solution)/shard_map/ppermute | solution.py:33
  210.5 10.6 %collective-permute-start.17 = (f32[1,2,256,128]{3,2,1,0:T(8,128)}, f32[1,2,256,128]{3,2,1,0:T(8,128)S(1)}, u32[]{:S(2)}, u32[]{:S(2)}) collective-permute-start(f32[1,2,256,128]{3,2,1,0:T(8,128)} %param.11), channel_id=1, source_target_pairs={{3,0},{4,1},{5,2},{6,3},{7,4},{8,5},{9,6},{10,7},{11,8},{12,9},{13... | collective-permute-start | bytes 786440 | tf_op jit(solution)/shard_map/ppermute | solution.py:33
  972.5 2.8 copy-start
where the time goes:
time: 999 us; the launch traced here: 980 us
  blocking collectives  836 us (84%)
  starting transfers between devices  80.4 us (8%)
  matrix products  27.6 us (3%)
  local copies, waits for them, and re-layouts  18.2 us (2%)
    psum x1, blocking collectives, body(): totals = lax.psum(jnp.sum(low_modes(present_state) ** 2, axis=0), 'dom')  725 us
    unnamed x1, blocking collectives  111 us
    ppermute x18, starting transfers between devices, from_behind(): lax.ppermute(value, axis, [(source, source + steps) for source in range(l...  80.4 us
  transfers between devices with their start and end apart: 18, of which 2 were waited for; matrix products, arithmetic and copies ran while one was open for 2% of the time, Pallas kernels for 0%

commit v1 on v0

--- a/solution.py
+++ b/solution.py
@@ -153,7 +153,7 @@
         (cand_start[None, :] <= slot_ids[:, None]) & (slot_ids[:, None] < cand_end[None, :])
     ).astype(jnp.float32)
     present_state = jnp.einsum("sc,cxyz->sxyz", chosen, candidates, precision=highest)
-    totals = lax.psum(jnp.sum(low_modes(present_state) ** 2, axis=0), "dom")
+    totals = jnp.sum(lax.all_gather(jnp.sum(low_modes(present_state) ** 2, axis=0), "dom"), axis=0)
     adapted = jnp.sqrt(totals / (per_device * devices) + 1e-06)
     wave_y, wave_x = wavenumbers(grid)
     prior = prior_amplitude / (1.0 + jnp.sqrt(wave_y * wave_y + wave_x * wave_x) / 8.0)

time: 999 us -> 1170 us (1.17); the launches traced: 980 us -> 1170 us
  waiting for transfers between devices: 9.8 us -> 908 us
  blocking collectives: 836 us -> 106 us
  between operations: 4.48 us -> 17.9 us
    all_gather x0 -> x1, waiting for transfers between devices: none -> 893 us  [body(): lax.all_gather(jnp.sum(low_modes(present_state) ** 2, axis=0), 'dom')]
    psum x1 -> x0, blocking collectives: 725 us -> none  [body(): totals = lax.psum(jnp.sum(low_modes(present_state) ** 2, axis=0), 'dom')]
  transfers between devices with their start and end apart: 18 -> 19, of which waited for: 2 -> 4; matrix products, arithmetic and copies ran while one was open for 2% -> 1% of each run, Pallas kernels for 0% -> 0%
where the time goes in v1:
time: 1170 us
  waiting for transfers between devices  908 us (78%)
  blocking collectives  106 us (9%)
  starting transfers between devices  86.3 us (7%)
  matrix products  27.5 us (2%)
  between operations  17.9 us (2%)
  local copies, waits for them, and re-layouts  14.3 us (1%)
    all_gather x1, waiting for transfers between devices, body(): lax.all_gather(jnp.sum(low_modes(present_state) ** 2, axis=0), 'dom')  893 us
    unnamed x1, blocking collectives  106 us
    ppermute x18, starting transfers between devices, from_behind(): lax.ppermute(value, axis, [(source, source + steps) for source in range(l...  86.3 us
  transfers between devices with their start and end apart: 19, of which 4 were waited for; matrix products, arithmetic and copies ran while one was open for 1% of the time, Pallas kernels for 0%

profile of v1, /device:TPU:1, one launch (start us, length us, event | category | flops | bytes accessed | tf_op | source)
XLA Modules:
  0.0 1167.5 jit_solution(10788840636994203056)
XLA Ops:
  7.2 4.5 collective-permute-start.12
  11.7 5.6 collective-permute-start.13
  18.1 106.4 %all-reduce = s32[512]{0:T(512)S(1)} all-reduce(s32[512]{0:T(512)S(1)} %dynamic-update-slice.8), channel_id=1, replica_groups=mesh['dom'=512] {'dom'}, use_global_device_ids=true, to_apply=%add | all-reduce | flops 512 | bytes 4096
  125.8 8.5 collective-permute-start.10
  135.7 7.5 collective-permute-start.14
  144.2 5.4 collective-permute-start.6
  149.6 2.7 collective-permute-start.7
  152.3 6.5 collective-permute-start.8
  160.1 7.6 collective-permute-start
  167.7 2.7 collective-permute-start.1
  170.4 3.8 concatenate.79
  174.2 5.9 collective-permute-start.2
  181.4 13.6 %collective-permute-start.4 = (f32[1]{0:T(128)}, f32[1]{0:T(128)}, u32[]{:S(2)}, u32[]{:S(2)}) collective-permute-start(f32[1]{0:T(128)} %convert_element_type.174), channel_id=1, source_target_pairs={{0,3},{1,4},{2,5},{3,6},{4,7},{5,8},{6,9},{7,10},{8,11},{9,12},{10... | collective-permute-start | bytes 20 | tf_op jit(solution)/shard_map/ppermute | solution.py:33
  197.6 4.5 collective-permute-done.5
  202.1 8.1 collective-permute-start.16
  210.2 3.8 concatenate.78
  215.6 10.1 collective-permute-done.17
  225.8 2.1 fusion
  232.5 892.6 %all-gather.2.cloned.1.call-done = f32[512,2,16,16]{3,2,1,0:T(8,128)} async-done(((f32[1,2,16,16]{3,2,1,0:T(8,128)}), f32[512,2,16,16]{3,2,1,0:T(8,128)}) %all-gather.2.cloned.1.call-update) | async-done | bytes 1048592 | tf_op jit(solution)/shard_map/all_gather | solution.py:156
  1125.1 4.0 reduce_sum.27
  1131.6 1.8 convolution_bitcast_fusion.1
  1133.3 1.8 convolution_bitcast_fusion
  1140.5 1.8 convolution_bitcast_fusion.3
  1142.2 2.0 convolution_bitcast_fusion.2
  (96 shorter events, 37.2 us)
Async XLA Ops:
  7.2 1117.9 %all-gather.2.cloned.1.call-start = ((), (), s32[]{:S(2)}) async-start(), calls=%async_computation | async-start | bytes 8404992 | tf_op jit(solution)/shard_map/all_gather | solution.py:156
  7.2 206.7 %collective-permute-start.12 = (f32[1,2,256,128]{3,2,1,0:T(8,128)}, f32[1,2,256,128]{3,2,1,0:T(8,128)S(1)}, u32[]{:S(2)}, u32[]{:S(2)}) collective-permute-start(f32[1,2,256,128]{3,2,1,0:T(8,128)} %param.11), channel_id=1, source_target_pairs={{0,1},{1,2},{2,3},{3,4},{4,5},{5,6},{6,7},{7,8},{8,9},{9,10},{10,1... | collective-permute-start | bytes 786440 | tf_op jit(solution)/shard_map/ppermute | solution.py:33
  11.7 203.6 %collective-permute-start.13 = (f32[1,2,256,128]{3,2,1,0:T(8,128)}, f32[1,2,256,128]{3,2,1,0:T(8,128)S(1)}, u32[]{:S(2)}, u32[]{:S(2)}) collective-permute-start(f32[1,2,256,128]{3,2,1,0:T(8,128)} %param.11), channel_id=1, source_target_pairs={{1,0},{2,1},{3,2},{4,3},{5,4},{6,5},{7,6},{8,7},{9,8},{10,9},{11,1... | collective-permute-start | bytes 786440 | tf_op jit(solution)/shard_map/ppermute | solution.py:33
  125.8 18.3 %collective-permute-start.10 = (f32[1]{0:T(128)}, f32[1]{0:T(128)}, u32[]{:S(2)}, u32[]{:S(2)}) collective-permute-start(f32[1]{0:T(128)} %convert_element_type.176), channel_id=1, source_target_pairs={{0,3},{1,4},{2,5},{3,6},{4,7},{5,8},{6,9},{7,10},{8,11},{9,12},{10... | collective-permute-start | bytes 20 | tf_op jit(solution)/shard_map/ppermute | solution.py:33
  134.4 15.2 %collective-permute-start.11 = (f32[1]{0:T(128)}, f32[1]{0:T(128)}, u32[]{:S(2)}, u32[]{:S(2)}) collective-permute-start(f32[1]{0:T(128)} %convert_element_type.176), channel_id=1, source_target_pairs={{3,0},{4,1},{5,2},{6,3},{7,4},{8,5},{9,6},{10,7},{11,8},{12,9},{13... | collective-permute-start | bytes 20 | tf_op jit(solution)/shard_map/ppermute | solution.py:33
  135.7 79.7 %collective-permute-start.14 = (f32[1,2,256,128]{3,2,1,0:T(8,128)}, f32[1,2,256,128]{3,2,1,0:T(8,128)S(1)}, u32[]{:S(2)}, u32[]{:S(2)}) collective-permute-start(f32[1,2,256,128]{3,2,1,0:T(8,128)} %param.11), channel_id=1, source_target_pairs={{0,2},{1,3},{2,4},{3,5},{4,6},{5,7},{6,8},{7,9},{8,10},{9,11},{10,... | collective-permute-start | bytes 786440 | tf_op jit(solution)/shard_map/ppermute | solution.py:33
  144.2 8.1 collective-permute-start.6
  149.6 9.2 collective-permute-start.7
  152.3 7.8 collective-permute-start.8
  158.8 8.9 collective-permute-start.9
  160.1 14.1 %collective-permute-start = (f32[1]{0:T(128)}, f32[1]{0:T(128)}, u32[]{:S(2)}, u32[]{:S(2)}) collective-permute-start(f32[1]{0:T(128)} %convert_element_type.174), channel_id=1, source_target_pairs={{0,1},{1,2},{2,3},{3,4},{4,5},{5,6},{6,7},{7,8},{8,9},{9,10},{10,1... | collective-permute-start | bytes 20 | tf_op jit(solution)/shard_map/ppermute | solution.py:33
  167.7 12.4 %collective-permute-start.1 = (f32[1]{0:T(128)}, f32[1]{0:T(128)}, u32[]{:S(2)}, u32[]{:S(2)}) collective-permute-start(f32[1]{0:T(128)} %convert_element_type.174), channel_id=1, source_target_pairs={{1,0},{2,1},{3,2},{4,3},{5,4},{6,5},{7,6},{8,7},{9,8},{10,9},{11,1... | collective-permute-start | bytes 20 | tf_op jit(solution)/shard_map/ppermute | solution.py:33
  174.2 7.2 collective-permute-start.2
  180.1 14.9 %collective-permute-start.3 = (f32[1]{0:T(128)}, f32[1]{0:T(128)}, u32[]{:S(2)}, u32[]{:S(2)}) collective-permute-start(f32[1]{0:T(128)} %convert_element_type.174), channel_id=1, source_target_pairs={{2,0},{3,1},{4,2},{5,3},{6,4},{7,5},{8,6},{9,7},{10,8},{11,9},{12,... | collective-permute-start | bytes 20 | tf_op jit(solution)/shard_map/ppermute | solution.py:33
  181.4 14.9 %collective-permute-start.4 = (f32[1]{0:T(128)}, f32[1]{0:T(128)}, u32[]{:S(2)}, u32[]{:S(2)}) collective-permute-start(f32[1]{0:T(128)} %convert_element_type.174), channel_id=1, source_target_pairs={{0,3},{1,4},{2,5},{3,6},{4,7},{5,8},{6,9},{7,10},{8,11},{9,12},{10... | collective-permute-start | bytes 20 | tf_op jit(solution)/shard_map/ppermute | solution.py:33
  195.0 7.1 collective-permute-start.5
  196.3 19.1 %collective-permute-start.15 = (f32[1,2,256,128]{3,2,1,0:T(8,128)}, f32[1,2,256,128]{3,2,1,0:T(8,128)S(1)}, u32[]{:S(2)}, u32[]{:S(2)}) collective-permute-start(f32[1,2,256,128]{3,2,1,0:T(8,128)} %param.11), channel_id=1, source_target_pairs={{2,0},{3,1},{4,2},{5,3},{6,4},{7,5},{8,6},{9,7},{10,8},{11,9},{12,... | collective-permute-start | bytes 786440 | tf_op jit(solution)/shard_map/ppermute | solution.py:33
  202.1 13.5 %collective-permute-start.16 = (f32[1,2,256,128]{3,2,1,0:T(8,128)}, f32[1,2,256,128]{3,2,1,0:T(8,128)S(1)}, u32[]{:S(2)}, u32[]{:S(2)}) collective-permute-start(f32[1,2,256,128]{3,2,1,0:T(8,128)} %param.11), channel_id=1, source_target_pairs={{0,3},{1,4},{2,5},{3,6},{4,7},{5,8},{6,9},{7,10},{8,11},{9,12},{10... | collective-permute-start | bytes 786440 | tf_op jit(solution)/shard_map/ppermute | solution.py:33
  213.9 11.8 %collective-permute-start.17 = (f32[1,2,256,128]{3,2,1,0:T(8,128)}, f32[1,2,256,128]{3,2,1,0:T(8,128)S(1)}, u32[]{:S(2)}, u32[]{:S(2)}) collective-permute-start(f32[1,2,256,128]{3,2,1,0:T(8,128)} %param.11), channel_id=1, source_target_pairs={{3,0},{4,1},{5,2},{6,3},{7,4},{8,5},{9,6},{10,7},{11,8},{12,9},{13... | collective-permute-start | bytes 786440 | tf_op jit(solution)/shard_map/ppermute | solution.py:33
  215.6 13.2 %copy-start.1 = (f32[2,1,2,256,128]{4,3,2,1,0:T(8,128)S(1)}, f32[2,1,2,256,128]{4,3,2,1,0:T(8,128)}, u32[]{:S(2)}) copy-start(f32[2,1,2,256,128]{4,3,2,1,0:T(8,128)} %param.13) | copy-start | bytes 1572868
  227.9 1.3 copy-start.2
  1152.7 2.8 copy-start
Sparse Core Ops, SparseCore 0:
  229.0 896.0 all-gather.1
